TPU v7x, 256 devices: a whole 4x4x8 slice. The times are simulated.
256 devices in a mesh: ulysses: 16 (over z, x_hi), blk: 16 (over y, x_lo, core).
Axes of the slice: x: 4 (x_hi: 2, x_lo: 2; x = x_hi * 2 + x_lo), y: 4, z: 8, core: 2. Of those that a mesh axis runs over, the one named last changes fastest.
Arguments:
- queries: bfloat16 [16, 1024, 4096], P('blk', 'ulysses'), may hold values from -6 to 6
- key_rows: bfloat16 [16, 1024, 1024], P('blk', 'ulysses'), may hold values from -6 to 6
- value_rows: bfloat16 [16, 1024, 1024], P('blk', 'ulysses'), may hold values from -6 to 6
- tile_segment: int32 [128], replicated, may hold values from 0 to 31, never falling along the last dimension, each value on 1 to 8 neighbouring positions
Outputs:
- attended: bfloat16 [16, 1024, 4096], P('blk', 'ulysses')
Inputs may be any that keep to these rules, and one draw needn't show every extreme that they name: `tile_segment`: segment numbers never fall along the sequence and each segment covers 1 to 8 tiles.
All inputs are finite; a program needn't handle non-finite values.
Results may differ from a plain program's by a relative error of at most 0.0045.
Values may be sent and summed in bfloat16 or wider, within the bound.
A program may use at most 64 MiB of HBM per device.

v0:
```python
import math
import jax
import jax.numpy as jnp
from jax import lax
from jax.sharding import PartitionSpec as P

HEAD_DIM = 128
TILE = 128
masked_score = -1e30


def side_by_side(arrays, axis, split_dim, concat_dim, along):
    widths = [a.shape[along] for a in arrays]
    both = jnp.concatenate(arrays, axis=along)
    whole = lax.all_to_all(both, axis, split_axis=split_dim, concat_axis=concat_dim, tiled=True)
    return tuple(jnp.split(whole, [sum(widths[:k]) for k in range(1, len(widths))], axis=along))


def partner_2(value, axis, bit):
    return lax.ppermute(value, axis, [(i, i ^ 1 << bit) for i in range(lax.axis_size(axis))])


def side_by_side_2(arrays, axis, dim, along):
    ends, at = ([], 0)
    for a in arrays[:-1]:
        at += a.shape[along]
        ends.append(at)
    both = jnp.concatenate(arrays, axis=along)
    return tuple(jnp.split(lax.all_gather(both, axis, axis=dim, tiled=True), ends, axis=along))


def segment_of(positions, tile_segment):
    tiles_total = tile_segment.shape[0]
    matches = (positions // TILE)[:, None] == jnp.arange(tiles_total, dtype=jnp.int32)[None, :]
    return jnp.sum(jnp.where(matches, tile_segment[None, :], 0), axis=1)


def visible(query_pos, query_seg, key_pos, key_seg):
    earlier = key_pos[None, :] <= query_pos[:, None]
    same_image = (key_seg[None, :] == query_seg[:, None]) & (query_seg[:, None] % 2 == 1)
    return earlier | same_image


def widen(source_rows, groups):
    tokens_dev = source_rows.shape[1]
    heads_here = source_rows.shape[2] // HEAD_DIM
    factor = max(1, groups // heads_here)
    spread = jnp.repeat(source_rows.reshape(1, tokens_dev, heads_here, HEAD_DIM), factor, axis=2)
    return spread.reshape(1, tokens_dev, heads_here * factor * HEAD_DIM)


def same_rows(row_ids):
    return row_ids


def update(current, allowed, query_block, key_block, value_block):
    maxima, denominators, weighted = current
    scores = jnp.einsum(
        "qkgd,skd->kgqs", query_block, key_block, preferred_element_type=jnp.float32
    )
    scores = jnp.where(allowed[None, None], scores * HEAD_DIM ** (-0.5), masked_score)
    new_max = jnp.maximum(maxima, jnp.max(scores, axis=3))
    weights = jnp.where(allowed[None, None], jnp.exp(scores - new_max[..., None]), 0.0)
    factor = jnp.exp(maxima - new_max)
    denominators = factor * denominators + jnp.sum(weights, axis=3)
    product = jnp.einsum(
        "kgqs,skd->kgqd",
        weights.astype(jnp.bfloat16),
        value_block,
        preferred_element_type=jnp.float32,
    )
    weighted = factor[..., None] * weighted + product
    return (new_max, denominators, weighted)


def keep_state(current, allowed, query_block, key_block, value_block):
    return current


def build_fold(query_rows, query_pos, tile_segment, key_position, kv_width):
    rows_total = query_rows.shape[0]
    kv_local = kv_width // HEAD_DIM
    group_size = query_rows.shape[1] // HEAD_DIM // kv_local
    shaped = query_rows.reshape(rows_total, kv_local, group_size, HEAD_DIM)
    query_seg = segment_of(query_pos, tile_segment)
    half_rows = rows_total // 2

    def fold_step(running, portion, offset):
        key_part, value_part = portion
        portion_rows = key_part.shape[0]
        block_rows = math.gcd(portion_rows, 512)
        block_total = portion_rows // block_rows
        key_blocks = key_part.reshape(block_total, block_rows, kv_local, HEAD_DIM)
        value_blocks = value_part.reshape(block_total, block_rows, kv_local, HEAD_DIM)

        def one_block(halves, inputs):
            key_block, value_block, block_number = inputs
            key_pos = key_position(
                block_number * block_rows + jnp.arange(block_rows, dtype=jnp.int32)
            )
            key_seg = segment_of(key_pos, tile_segment)
            results = []
            for half_index in range(2):
                row_low = half_index * half_rows
                row_high = row_low + half_rows
                allowed = visible(
                    query_pos[row_low:row_high], query_seg[row_low:row_high], key_pos, key_seg
                )
                results.append(
                    lax.cond(
                        jnp.any(allowed),
                        update,
                        keep_state,
                        halves[half_index],
                        allowed,
                        shaped[row_low:row_high],
                        key_block,
                        value_block,
                    )
                )
            return ((results[0], results[1]), None)

        running, unused = lax.scan(
            one_block, running, (key_blocks, value_blocks, jnp.arange(block_total, dtype=jnp.int32))
        )
        return running

    def empty_half():
        return (
            jnp.full((kv_local, group_size, half_rows), masked_score, jnp.float32),
            jnp.zeros((kv_local, group_size, half_rows), jnp.float32),
            jnp.zeros((kv_local, group_size, half_rows, HEAD_DIM), jnp.float32),
        )

    return (fold_step, (empty_half(), empty_half()))


def finish(running):
    outputs = [weighted / denominators[..., None] for maxima, denominators, weighted in running]
    joined = jnp.concatenate(outputs, axis=2)
    kv_local, group_size, rows_total, head_dim = joined.shape
    joined = jnp.transpose(joined, (2, 0, 1, 3)).reshape(
        rows_total, kv_local * group_size * head_dim
    )
    return joined.astype(jnp.bfloat16)


def local(queries, key_rows, value_rows, tile_segment):
    ulysses_count = lax.axis_size("ulysses")
    block_count = lax.axis_size("blk")
    tokens_dev = queries.shape[1]
    block_len = tokens_dev * ulysses_count
    block_index = lax.axis_index("blk")
    local_rows = jnp.arange(block_len, dtype=jnp.int32)
    moved = (
        lax.all_to_all(queries, "ulysses", split_axis=2, concat_axis=1, tiled=True),
        *side_by_side(
            (widen(key_rows, ulysses_count), widen(value_rows, ulysses_count)), "ulysses", 2, 1, 0
        ),
    )
    query_rows, key_local, value_local = (moved[0][0], moved[1][0], moved[2][0])
    half_rows = block_len // 2
    partner = block_count - 1 - block_index
    travelling = query_rows[half_rows:]
    for bit_index in range(block_count.bit_length() - 1):
        travelling = partner_2(travelling, "blk", bit_index)
    query_rows = jnp.concatenate([query_rows[:half_rows], travelling], axis=0)
    query_pos = jnp.concatenate(
        [
            block_index * block_len + local_rows[:half_rows],
            partner * block_len + local_rows[half_rows:],
        ]
    )
    fold_step, initial = build_fold(
        query_rows, query_pos, tile_segment, same_rows, key_local.shape[1]
    )
    running = fold_step(
        initial, side_by_side_2((key_local, value_local), "blk", 0, 1), jnp.int32(0)
    )
    out_rows = finish(running)
    returning = out_rows[half_rows:]
    for bit_index in range(block_count.bit_length() - 1):
        returning = partner_2(returning, "blk", bit_index)
    out_rows = jnp.concatenate([out_rows[:half_rows], returning], axis=0)
    attended = lax.all_to_all(out_rows[None], "ulysses", split_axis=1, concat_axis=2, tiled=True)
    return attended


def solution(mesh):
    return jax.shard_map(
        local,
        mesh=mesh,
        in_specs=(
            P("blk", "ulysses", None),
            P("blk", "ulysses", None),
            P("blk", "ulysses", None),
            P(),
        ),
        out_specs=P("blk", "ulysses", None),
        check_vma=False,
    )
```

profile of v0, /device:TPU:16, one launch (start us, length us, event | category | flops | bytes accessed | tf_op | source)
XLA Modules:
  0.0 428.8 jit_solution(16484188474409896511)
XLA Ops:
  10.6 29.6 %all_to_all.48 = bf16[16,2,8192]{2,1,0:T(2,128)(2,1)S(1)} all-to-all(bf16[16,2,8192]{2,1,0:T(2,128)(2,1)S(1)} %reshape.218), channel_id=1, replica_groups=mesh['ulysses'=16,'blk'=16] {'ulysses'}, dimensions={0} | all-to-all | bytes 1048576 | tf_op jit(solution)/shard_map/all_to_all | solution.py:15
  42.7 2.8 copy.75
  46.1 22.5 %reduce.4 = bf16[4096,64]{1,0:T(8,128)(2,1)S(1)} reduce(bf16[4096,1,64]{2,1,0:T(2,128)(2,1)S(1)} %bitcast.147, bf16[]{:T(256)} %broadcast.213), dimensions={1}, to_apply=%bitcast.127.reduce_sub_computation | reduce | bytes 1048578
  69.3 22.1 %all_to_all.49 = bf16[16,2,8192]{2,1,0:T(2,128)(2,1)S(1)} all-to-all(bf16[16,2,8192]{2,1,0:T(2,128)(2,1)S(1)} %reshape.220), channel_id=1, replica_groups=mesh['ulysses'=16,'blk'=16] {'ulysses'}, dimensions={0} | all-to-all | bytes 1048576 | tf_op jit(solution)/shard_map/all_to_all | solution.py:156
  92.6 2.3 copy.76
  95.3 1.5 collective-permute-done
  97.4 7.8 %collective-permute-done.1 = bf16[512,256]{1,0:T(8,128)(2,1)S(1)} collective-permute-done((bf16[512,256]{1,0:T(8,128)(2,1)S(1)}, bf16[512,256]{1,0:T(8,128)(2,1)S(1)}, u32[]{:S(2)}, u32[]{:S(2)}) %collective-permute-start.1) | collective-permute-done | bytes 262176 | tf_op jit(solution)/shard_map/ppermute | solution.py:20
  105.1 1.3 collective-permute-start.2
  106.5 6.1 %collective-permute-done.2 = bf16[512,256]{1,0:T(8,128)(2,1)S(1)} collective-permute-done((bf16[512,256]{1,0:T(8,128)(2,1)S(1)}, bf16[512,256]{1,0:T(8,128)(2,1)S(1)}, u32[]{:S(2)}, u32[]{:S(2)}) %collective-permute-start.2) | collective-permute-done | bytes 262176 | tf_op jit(solution)/shard_map/ppermute | solution.py:20
  113.5 7.3 %collective-permute-done.3 = bf16[512,256]{1,0:T(8,128)(2,1)S(1)} collective-permute-done((bf16[512,256]{1,0:T(8,128)(2,1)S(1)}, bf16[512,256]{1,0:T(8,128)(2,1)S(1)}, u32[]{:S(2)}, u32[]{:S(2)}) %collective-permute-start.3) | collective-permute-done | bytes 262176 | tf_op jit(solution)/shard_map/ppermute | solution.py:20
  121.9 5.7 %fusion.52 = (bf16[16384,128]{1,0:T(8,128)(2,1)}, bf16[16384,128]{1,0:T(8,128)(2,1)}) fusion(bf16[16384,256]{1,0:T(8,128)(2,1)} %all-gather.2.cloned.1.call-done), kind=kLoop, calls=%fused_computation.100 | loop fusion | bytes 16777216 | tf_op jit(solution)/shard_map/split | solution.py:29
  127.7 236.1 %while.23 = (s32[]{:T(128)}, f32[1,2,512]{2,1,0:T(2,128)S(1)}, f32[1,2,512]{2,1,0:T(2,128)S(1)}, f32[1,2,512,128]{3,2,1,0:T(8,128)S(1)}, f32[1,2,512]{2,1,0:T(2,...) while((s32[]{:T(128)}, f32[1,2,512]{2,1,0:T(2,128)S(1)}, ...), condition=%wide.region_13.14_spmd, body=%wide.region_1.13_spmd.sunk | while | flops 553869824 | bytes 18521024 | solution.py:123
  130.2 1.3 fusion.61
  132.8 2.2 conditional.5
  134.9 2.2 conditional.4
  139.6 1.3 fusion.61
  142.1 2.2 conditional.5
  144.3 2.2 conditional.4
  151.5 2.2 conditional.5
  153.7 2.2 conditional.4
  158.4 1.3 fusion.61
  160.9 2.2 conditional.5
  163.1 2.2 conditional.4
  170.3 2.2 conditional.5
  172.4 2.2 conditional.4
  177.1 1.3 fusion.61
  179.7 2.2 conditional.5
  181.8 2.2 conditional.4
  186.5 1.3 fusion.61
  189.0 2.2 conditional.5
  191.2 2.2 conditional.4
  198.4 2.2 conditional.5
  200.6 2.2 conditional.4
  205.3 1.3 fusion.61
  207.8 2.2 conditional.5
  210.0 2.2 conditional.4
  214.7 1.3 fusion.61
  217.2 2.2 conditional.5
  219.3 2.2 conditional.4
  226.6 2.2 conditional.5
  228.7 2.2 conditional.4
  233.4 1.3 fusion.61
  235.9 2.2 conditional.5
  238.1 2.2 conditional.4
  242.8 1.3 fusion.61
  245.3 2.2 conditional.5
  247.5 2.2 conditional.4
  252.2 1.3 fusion.61
  254.7 2.2 conditional.5
  256.9 2.2 conditional.4
  261.6 1.3 fusion.61
  264.1 2.2 conditional.5
  266.3 2.2 conditional.4
  273.5 2.2 conditional.5
  275.6 2.2 conditional.4
  282.9 2.2 conditional.4
  290.1 2.2 conditional.4
  364.6 1.5 collective-permute-done.4
  366.1 8.3 %collective-permute-done.5 = bf16[512,256]{0,1:T(8,128)(2,1)S(1)} collective-permute-done((bf16[512,256]{0,1:T(8,128)(2,1)S(1)}, bf16[512,256]{0,1:T(8,128)(2,1)S(1)}, u32[]{:S(2)}, u32[]{:S(2)}) %collective-permute-start.5) | collective-permute-done | bytes 262176 | tf_op jit(solution)/shard_map/ppermute | solution.py:20
  374.4 3.5 collective-permute-start.6
  377.9 5.7 %collective-permute-done.6 = bf16[512,256]{0,1:T(8,128)(2,1)S(1)} collective-permute-done((bf16[512,256]{0,1:T(8,128)(2,1)S(1)}, bf16[512,256]{0,1:T(8,128)(2,1)S(1)}, u32[]{:S(2)}, u32[]{:S(2)}) %collective-permute-start.6) | collective-permute-done | bytes 262176 | tf_op jit(solution)/shard_map/ppermute | solution.py:20
  384.4 7.7 %collective-permute-done.7 = bf16[512,256]{0,1:T(8,128)(2,1)S(1)} collective-permute-done((bf16[512,256]{0,1:T(8,128)(2,1)S(1)}, bf16[512,256]{0,1:T(8,128)(2,1)S(1)}, u32[]{:S(2)}, u32[]{:S(2)}) %collective-permute-start.7) | collective-permute-done | bytes 262176 | tf_op jit(solution)/shard_map/ppermute | solution.py:20
  393.0 3.9 reduce.5
  397.0 23.5 %all_to_all.50 = bf16[16,2,8192]{2,1,0:T(2,128)(2,1)S(1)} all-to-all(bf16[16,2,8192]{2,1,0:T(2,128)(2,1)S(1)} %reshape.222), channel_id=1, replica_groups=mesh['ulysses'=16,'blk'=16] {'ulysses'}, dimensions={0} | all-to-all | bytes 1048576 | tf_op jit(solution)/shard_map/all_to_all | solution.py:185
  (513 shorter events, 174.4 us)
Async XLA Ops:
  6.5 115.3 %all-gather.2.cloned.1.call-start = ((), (), s32[]{:S(2)}) async-start(), calls=%async_computation.3 | async-start | bytes 8912896 | tf_op jit(solution)/shard_map/all_gather | solution.py:29
  41.7 1.1 copy-start
  94.9 18.1 %copy-start.1 = (s32[128]{0:T(128)S(1)}, s32[128]{0:T(128)}, u32[]{:S(2)}) copy-start(s32[128]{0:T(128)} %param.13) | copy-start | bytes 1540
  95.2 1.6 collective-permute-start
  96.8 8.3 %collective-permute-start.1 = (bf16[512,256]{1,0:T(8,128)(2,1)S(1)}, bf16[512,256]{1,0:T(8,128)(2,1)S(1)}, u32[]{:S(2)}, u32[]{:S(2)}) collective-permute-start(bf16[512,256]{1,0:T(8,128)(2,1)S(1)} %collective-permute-done), channel_id=1, source_target_pairs={{0,2},{1,3},{2,0},{3,1},{4,6},{5,7},{6,4},{7,5},{8,10},{9,11},{10,... | collective-permute-start | bytes 786440 | tf_op jit(solution)/shard_map/ppermute | solution.py:20
  105.1 7.5 %collective-permute-start.2 = (bf16[512,256]{1,0:T(8,128)(2,1)S(1)}, bf16[512,256]{1,0:T(8,128)(2,1)S(1)}, u32[]{:S(2)}, u32[]{:S(2)}) collective-permute-start(bf16[512,256]{1,0:T(8,128)(2,1)S(1)} %collective-permute-done.1), channel_id=1, source_target_pairs={{0,4},{1,5},{2,6},{3,7},{4,0},{5,1},{6,2},{7,3},{8,12},{9,13},{10,... | collective-permute-start | bytes 786440 | tf_op jit(solution)/shard_map/ppermute | solution.py:20
  112.6 8.1 %collective-permute-start.3 = (bf16[512,256]{1,0:T(8,128)(2,1)S(1)}, bf16[512,256]{1,0:T(8,128)(2,1)S(1)}, u32[]{:S(2)}, u32[]{:S(2)}) collective-permute-start(bf16[512,256]{1,0:T(8,128)(2,1)S(1)} %collective-permute-done.2), channel_id=1, source_target_pairs={{0,8},{1,9},{2,10},{3,11},{4,12},{5,13},{6,14},{7,15},{8,0},{9,1},... | collective-permute-start | bytes 786440 | tf_op jit(solution)/shard_map/ppermute | solution.py:20
  364.5 1.6 collective-permute-start.4
  366.1 8.3 %collective-permute-start.5 = (bf16[512,256]{0,1:T(8,128)(2,1)S(1)}, bf16[512,256]{0,1:T(8,128)(2,1)S(1)}, u32[]{:S(2)}, u32[]{:S(2)}) collective-permute-start(bf16[512,256]{0,1:T(8,128)(2,1)S(1)} %collective-permute-done.4), channel_id=1, source_target_pairs={{0,2},{1,3},{2,0},{3,1},{4,6},{5,7},{6,4},{7,5},{8,10},{9,11},{10,... | collective-permute-start | bytes 786440 | tf_op jit(solution)/shard_map/ppermute | solution.py:20
  374.4 9.3 %collective-permute-start.6 = (bf16[512,256]{0,1:T(8,128)(2,1)S(1)}, bf16[512,256]{0,1:T(8,128)(2,1)S(1)}, u32[]{:S(2)}, u32[]{:S(2)}) collective-permute-start(bf16[512,256]{0,1:T(8,128)(2,1)S(1)} %collective-permute-done.5), channel_id=1, source_target_pairs={{0,4},{1,5},{2,6},{3,7},{4,0},{5,1},{6,2},{7,3},{8,12},{9,13},{10,... | collective-permute-start | bytes 786440 | tf_op jit(solution)/shard_map/ppermute | solution.py:20
  383.7 8.4 %collective-permute-start.7 = (bf16[512,256]{0,1:T(8,128)(2,1)S(1)}, bf16[512,256]{0,1:T(8,128)(2,1)S(1)}, u32[]{:S(2)}, u32[]{:S(2)}) collective-permute-start(bf16[512,256]{0,1:T(8,128)(2,1)S(1)} %collective-permute-done.6), channel_id=1, source_target_pairs={{0,8},{1,9},{2,10},{3,11},{4,12},{5,13},{6,14},{7,15},{8,0},{9,1},... | collective-permute-start | bytes 786440 | tf_op jit(solution)/shard_map/ppermute | solution.py:20
Sparse Core Ops, SparseCore 0:
  42.9 53.3 all-gather.1
where the time goes:
time: 431 us; the launch traced here: 429 us
  other arithmetic  99.3 us (23%)
  blocking collectives  75.2 us (17%)
  local copies, waits for them, and re-layouts  73.2 us (17%)
  loops' own time  63.6 us (15%)
  matrix products  50.9 us (12%)
  waiting for transfers between devices  46 us (11%)
  between operations  13.8 us (3%)
  starting transfers between devices  6.73 us (2%)
    another operation x1, loops' own time, fold_step(): lax.scan(one_block, running, (key_blocks, value_blocks, jnp.arange(block_...  61.4 us
    ppermute x8, waiting for transfers between devices, partner_2(): lax.ppermute(value, axis, [(i, i ^ 1 << bit) for i in range(lax.axis_size...  46 us
    reduce_or x32, other arithmetic, one_block(): jnp.any(allowed)  41.9 us
    dot_general x34, matrix products, update(): jnp.einsum('kgqs,skd->kgqd', weights.astype(jnp.bfloat16), value_block, p...  32.1 us
    squeeze x32, local copies, waits for them, and re-layouts, fold_step(): lax.scan(one_block, running, (key_blocks, value_blocks, jnp.arange(block_...  31.8 us
    all_to_all x1, blocking collectives, side_by_side(): lax.all_to_all(both, axis, split_axis=split_dim, concat_axis=concat_dim,...  29.6 us
    unnamed x2, other arithmetic  26.3 us
    all_to_all x1, blocking collectives, local(): lax.all_to_all(out_rows[None], 'ulysses', split_axis=1, concat_axis=2, ti...  23.5 us
  transfers between devices with their start and end apart: 9, of which 8 were waited for; matrix products, arithmetic and copies ran while one was open for 7% of the time, Pallas kernels for 0%

commit v1 on v0

--- a/solution.py
+++ b/solution.py
@@ -153,7 +153,12 @@
     block_index = lax.axis_index("blk")
     local_rows = jnp.arange(block_len, dtype=jnp.int32)
     moved = (
-        lax.all_to_all(queries, "ulysses", split_axis=2, concat_axis=1, tiled=True),
+        jnp.concatenate(
+            lax.all_to_all(
+                jnp.stack(jnp.split(queries, lax.axis_size("ulysses"), axis=2)), "ulysses", 0, 0
+            ),
+            axis=1,
+        ),
         *side_by_side(
             (widen(key_rows, ulysses_count), widen(value_rows, ulysses_count)), "ulysses", 2, 1, 0
         ),

time: 431 us -> 420 us (0.974)
  other arithmetic: 99.3 us -> 76.6 us
  waiting for transfers between devices: 46 us -> 60.7 us
  local copies, waits for them, and re-layouts: 73.2 us -> 65.8 us
    unnamed x2 -> x1, other arithmetic: 26.3 us -> 3.82 us
    ppermute x8, waiting for transfers between devices: 46 us -> 59.4 us  [partner_2(): lax.ppermute(value, axis, [(i, i ^ 1 << bit) for i in range(lax.axis_size...]
    unnamed x16 -> x27, local copies, waits for them, and re-layouts: 9.37 us -> 4.57 us
  transfers between devices with their start and end apart: 9 -> 9, of which waited for: 8 -> 9; matrix products, arithmetic and copies ran while one was open for 7% -> 0% of each run, Pallas kernels for 0% -> 0%
where the time goes in v1:
time: 420 us; the launch traced here: 418 us
  blocking collectives  77.2 us (18%)
  other arithmetic  76.6 us (18%)
  local copies, waits for them, and re-layouts  65.8 us (16%)
  loops' own time  63.3 us (15%)
  waiting for transfers between devices  60.7 us (14%)
  matrix products  51.1 us (12%)
  between operations  13.9 us (3%)
  starting transfers between devices  9.37 us (2%)
    another operation x1, loops' own time, fold_step(): lax.scan(one_block, running, (key_blocks, value_blocks, jnp.arange(block_...  61.4 us
    ppermute x8, waiting for transfers between devices, partner_2(): lax.ppermute(value, axis, [(i, i ^ 1 << bit) for i in range(lax.axis_size...  59.4 us
    reduce_or x32, other arithmetic, one_block(): jnp.any(allowed)  41.9 us
    dot_general x34, matrix products, update(): jnp.einsum('kgqs,skd->kgqd', weights.astype(jnp.bfloat16), value_block, p...  32.3 us
    squeeze x32, local copies, waits for them, and re-layouts, fold_step(): lax.scan(one_block, running, (key_blocks, value_blocks, jnp.arange(block_...  31.5 us
    all_to_all x1, blocking collectives, side_by_side(): lax.all_to_all(both, axis, split_axis=split_dim, concat_axis=concat_dim,...  29.6 us
    all_to_all x1, blocking collectives, local(): lax.all_to_all(out_rows[None], 'ulysses', split_axis=1, concat_axis=2, ti...  25.5 us
    all_to_all x1, blocking collectives, local(): lax.all_to_all(jnp.stack(jnp.split(queries, lax.axis_size('ulysses'), axi...  22.1 us
  transfers between devices with their start and end apart: 9, of which 9 were waited for; matrix products, arithmetic and copies ran while one was open for 0% of the time, Pallas kernels for 0%

profile of v1, /device:TPU:16, one launch (start us, length us, event | category | flops | bytes accessed | tf_op | source)
XLA Modules:
  0.0 418.0 jit_solution(6411658175752980964)
XLA Ops:
  10.6 29.6 %all_to_all.38 = bf16[16,2,8192]{2,1,0:T(2,128)(2,1)S(1)} all-to-all(bf16[16,2,8192]{2,1,0:T(2,128)(2,1)S(1)} %reshape.217), channel_id=1, replica_groups=mesh['ulysses'=16,'blk'=16] {'ulysses'}, dimensions={0} | all-to-all | bytes 1048576 | tf_op jit(solution)/shard_map/all_to_all | solution.py:15
  43.0 22.1 %all_to_all.39 = bf16[16,1,64,256]{3,2,1,0:T(8,128)(2,1)S(1)} all-to-all(bf16[16,1,64,256]{3,2,1,0:T(8,128)(2,1)S(1)} %constant_dynamic-update-slice_fusion), channel_id=1, replica_groups=mesh['ulysses'=16,'blk'=16] {'ulysses'}, dimensions={0} | all-to-all | bytes 1048576 | tf_op jit(solution)/shard_map/all_to_all | solution.py:157
  65.2 1.5 collective-permute-done
  67.3 7.8 %collective-permute-done.1 = bf16[512,256]{1,0:T(8,128)(2,1)S(1)} collective-permute-done((bf16[512,256]{1,0:T(8,128)(2,1)S(1)}, bf16[512,256]{1,0:T(8,128)(2,1)S(1)}, u32[]{:S(2)}, u32[]{:S(2)}) %collective-permute-start.1) | collective-permute-done | bytes 262176 | tf_op jit(solution)/shard_map/ppermute | solution.py:20
  75.1 7.7 %collective-permute-start.2 = (bf16[512,256]{1,0:T(8,128)(2,1)S(1)}, bf16[512,256]{1,0:T(8,128)(2,1)S(1)}, u32[]{:S(2)}, u32[]{:S(2)}) collective-permute-start(bf16[512,256]{1,0:T(8,128)(2,1)S(1)} %collective-permute-done.1), channel_id=1, source_target_pairs={{0,4},{1,5},{2,6},{3,7},{4,0},{5,1},{6,2},{7,3},{8,12},{9,13},{10,... | collective-permute-start | bytes 786440 | tf_op jit(solution)/shard_map/ppermute | solution.py:20
  82.8 11.9 %collective-permute-done.2 = bf16[512,256]{1,0:T(8,128)(2,1)S(1)} collective-permute-done((bf16[512,256]{1,0:T(8,128)(2,1)S(1)}, bf16[512,256]{1,0:T(8,128)(2,1)S(1)}, u32[]{:S(2)}, u32[]{:S(2)}) %collective-permute-start.2) | collective-permute-done | bytes 262176 | tf_op jit(solution)/shard_map/ppermute | solution.py:20
  95.1 13.6 %collective-permute-done.3 = bf16[512,256]{1,0:T(8,128)(2,1)S(1)} collective-permute-done((bf16[512,256]{1,0:T(8,128)(2,1)S(1)}, bf16[512,256]{1,0:T(8,128)(2,1)S(1)}, u32[]{:S(2)}, u32[]{:S(2)}) %collective-permute-start.3) | collective-permute-done | bytes 262176 | tf_op jit(solution)/shard_map/ppermute | solution.py:20
  111.1 5.7 %fusion.52 = (bf16[16384,128]{1,0:T(8,128)(2,1)}, bf16[16384,128]{1,0:T(8,128)(2,1)}) fusion(bf16[16384,256]{1,0:T(8,128)(2,1)} %all-gather.2.cloned.1.call-done), kind=kLoop, calls=%fused_computation.115 | loop fusion | bytes 16777216 | tf_op jit(solution)/shard_map/split | solution.py:29
  116.9 235.6 %while.23 = (s32[]{:T(128)}, f32[1,2,512]{2,1,0:T(2,128)S(1)}, f32[1,2,512]{2,1,0:T(2,128)S(1)}, f32[1,2,512,128]{3,2,1,0:T(8,128)S(1)}, f32[1,2,512]{2,1,0:T(2,...) while((s32[]{:T(128)}, f32[1,2,512]{2,1,0:T(2,128)S(1)}, ...), condition=%wide.region_13.14_spmd, body=%wide.region_1.13_spmd.sunk | while | flops 553869824 | bytes 18521016 | solution.py:123
  118.5 1.3 fusion.60
  121.4 2.2 conditional.5
  124.1 2.2 conditional.4
  127.8 1.3 fusion.60
  130.8 2.2 conditional.5
  133.5 2.2 conditional.4
  137.2 1.3 fusion.60
  140.2 2.2 conditional.5
  142.9 2.2 conditional.4
  146.6 1.3 fusion.60
  149.5 2.2 conditional.5
  152.2 2.2 conditional.4
  155.9 1.3 fusion.60
  158.9 2.2 conditional.5
  161.6 2.2 conditional.4
  165.3 1.3 fusion.60
  168.2 2.2 conditional.5
  171.0 2.2 conditional.4
  174.7 1.3 fusion.60
  177.6 2.2 conditional.5
  180.3 2.2 conditional.4
  184.0 1.3 fusion.60
  187.0 2.2 conditional.5
  189.7 2.2 conditional.4
  196.3 2.2 conditional.5
  199.1 2.2 conditional.4
  202.8 1.3 fusion.60
  205.7 2.2 conditional.5
  208.4 2.2 conditional.4
  215.1 2.2 conditional.5
  217.8 2.2 conditional.4
  221.5 1.3 fusion.60
  224.4 2.2 conditional.5
  227.1 2.2 conditional.4
  233.8 2.2 conditional.5
  236.5 2.2 conditional.4
  240.2 1.3 fusion.60
  243.2 2.2 conditional.5
  245.9 2.2 conditional.4
  252.5 2.2 conditional.5
  255.2 2.2 conditional.4
  258.9 1.3 fusion.60
  261.9 2.2 conditional.5
  264.6 2.2 conditional.4
  271.8 2.2 conditional.4
  275.5 1.3 fusion.60
  279.1 2.2 conditional.4
  282.8 1.3 fusion.60
  292.9 1.3 fusion.60
  353.2 1.5 collective-permute-done.4
  354.8 8.3 %collective-permute-done.5 = bf16[512,256]{0,1:T(8,128)(2,1)S(1)} collective-permute-done((bf16[512,256]{0,1:T(8,128)(2,1)S(1)}, bf16[512,256]{0,1:T(8,128)(2,1)S(1)}, u32[]{:S(2)}, u32[]{:S(2)}) %collective-permute-start.5) | collective-permute-done | bytes 262176 | tf_op jit(solution)/shard_map/ppermute | solution.py:20
  363.3 7.3 %collective-permute-done.6 = bf16[512,256]{0,1:T(8,128)(2,1)S(1)} collective-permute-done((bf16[512,256]{0,1:T(8,128)(2,1)S(1)}, bf16[512,256]{0,1:T(8,128)(2,1)S(1)}, u32[]{:S(2)}, u32[]{:S(2)}) %collective-permute-start.6) | collective-permute-done | bytes 262176 | tf_op jit(solution)/shard_map/ppermute | solution.py:20
  371.3 7.4 %collective-permute-done.7 = bf16[512,256]{0,1:T(8,128)(2,1)S(1)} collective-permute-done((bf16[512,256]{0,1:T(8,128)(2,1)S(1)}, bf16[512,256]{0,1:T(8,128)(2,1)S(1)}, u32[]{:S(2)}, u32[]{:S(2)}) %collective-permute-start.7) | collective-permute-done | bytes 262176 | tf_op jit(solution)/shard_map/ppermute | solution.py:20
  380.2 3.8 reduce.4
  384.1 25.5 %all_to_all.40 = bf16[16,2,8192]{2,1,0:T(2,128)(2,1)S(1)} all-to-all(bf16[16,2,8192]{2,1,0:T(2,128)(2,1)S(1)} %reshape.219), channel_id=1, replica_groups=mesh['ulysses'=16,'blk'=16] {'ulysses'}, dimensions={0} | all-to-all | bytes 1048576 | tf_op jit(solution)/shard_map/all_to_all | solution.py:190
  (521 shorter events, 167.8 us)
Async XLA Ops:
  6.5 104.6 %all-gather.2.cloned.1.call-start = ((), (), s32[]{:S(2)}) async-start(), calls=%async_computation.3 | async-start | bytes 8912896 | tf_op jit(solution)/shard_map/all_gather | solution.py:29
  41.7 1.1 copy-start
  41.9 52.8 %copy-start.1 = (s32[128]{0:T(128)S(1)}, s32[128]{0:T(128)}, u32[]{:S(2)}) copy-start(s32[128]{0:T(128)} %param.13) | copy-start | bytes 1540
  65.1 1.6 collective-permute-start
  66.7 8.3 %collective-permute-start.1 = (bf16[512,256]{1,0:T(8,128)(2,1)S(1)}, bf16[512,256]{1,0:T(8,128)(2,1)S(1)}, u32[]{:S(2)}, u32[]{:S(2)}) collective-permute-start(bf16[512,256]{1,0:T(8,128)(2,1)S(1)} %collective-permute-done), channel_id=1, source_target_pairs={{0,2},{1,3},{2,0},{3,1},{4,6},{5,7},{6,4},{7,5},{8,10},{9,11},{10,... | collective-permute-start | bytes 786440 | tf_op jit(solution)/shard_map/ppermute | solution.py:20
  75.1 19.6 %collective-permute-start.2 = (bf16[512,256]{1,0:T(8,128)(2,1)S(1)}, bf16[512,256]{1,0:T(8,128)(2,1)S(1)}, u32[]{:S(2)}, u32[]{:S(2)}) collective-permute-start(bf16[512,256]{1,0:T(8,128)(2,1)S(1)} %collective-permute-done.1), channel_id=1, source_target_pairs={{0,4},{1,5},{2,6},{3,7},{4,0},{5,1},{6,2},{7,3},{8,12},{9,13},{10,... | collective-permute-start | bytes 786440 | tf_op jit(solution)/shard_map/ppermute | solution.py:20
  94.6 14.1 %collective-permute-start.3 = (bf16[512,256]{1,0:T(8,128)(2,1)S(1)}, bf16[512,256]{1,0:T(8,128)(2,1)S(1)}, u32[]{:S(2)}, u32[]{:S(2)}) collective-permute-start(bf16[512,256]{1,0:T(8,128)(2,1)S(1)} %collective-permute-done.2), channel_id=1, source_target_pairs={{0,8},{1,9},{2,10},{3,11},{4,12},{5,13},{6,14},{7,15},{8,0},{9,1},... | collective-permute-start | bytes 786440 | tf_op jit(solution)/shard_map/ppermute | solution.py:20
  353.1 1.6 collective-permute-start.4
  354.8 8.3 %collective-permute-start.5 = (bf16[512,256]{0,1:T(8,128)(2,1)S(1)}, bf16[512,256]{0,1:T(8,128)(2,1)S(1)}, u32[]{:S(2)}, u32[]{:S(2)}) collective-permute-start(bf16[512,256]{0,1:T(8,128)(2,1)S(1)} %collective-permute-done.4), channel_id=1, source_target_pairs={{0,2},{1,3},{2,0},{3,1},{4,6},{5,7},{6,4},{7,5},{8,10},{9,11},{10,... | collective-permute-start | bytes 786440 | tf_op jit(solution)/shard_map/ppermute | solution.py:20
  363.1 7.5 %collective-permute-start.6 = (bf16[512,256]{0,1:T(8,128)(2,1)S(1)}, bf16[512,256]{0,1:T(8,128)(2,1)S(1)}, u32[]{:S(2)}, u32[]{:S(2)}) collective-permute-start(bf16[512,256]{0,1:T(8,128)(2,1)S(1)} %collective-permute-done.5), channel_id=1, source_target_pairs={{0,4},{1,5},{2,6},{3,7},{4,0},{5,1},{6,2},{7,3},{8,12},{9,13},{10,... | collective-permute-start | bytes 786440 | tf_op jit(solution)/shard_map/ppermute | solution.py:20
  370.6 8.1 %collective-permute-start.7 = (bf16[512,256]{0,1:T(8,128)(2,1)S(1)}, bf16[512,256]{0,1:T(8,128)(2,1)S(1)}, u32[]{:S(2)}, u32[]{:S(2)}) collective-permute-start(bf16[512,256]{0,1:T(8,128)(2,1)S(1)} %collective-permute-done.6), channel_id=1, source_target_pairs={{0,8},{1,9},{2,10},{3,11},{4,12},{5,13},{6,14},{7,15},{8,0},{9,1},... | collective-permute-start | bytes 786440 | tf_op jit(solution)/shard_map/ppermute | solution.py:20
Sparse Core Ops, SparseCore 0:
  42.9 68.1 all-gather.1
